TPU v7x, 32 devices: a whole 2x2x4 slice. The times are simulated.
32 devices in a mesh: dp: 8 (over z, y), tensor: 4 (over x, core).
Axes of the slice: x: 2, y: 2, z: 4, core: 2. Of those that a mesh axis runs over, the one named last changes fastest.
Arguments:
- tokens: bfloat16 [8192, 1024], P('dp'), may hold values from -6 to 6
- cotangent: bfloat16 [8192, 1024], P('dp'), may hold values from -6 to 6
- norm_params: float32 [4, 1024], replicated, may hold values from 0.25 to 1.75
- attention_weight: bfloat16 [1024, 3, 1024], P('dp', None, 'tensor'), may hold values from -0.1875 to 0.1875
- attention_bias: float32 [3, 1024], P(None, 'tensor'), may hold values from -3 to 3
- merge_weight: bfloat16 [1024, 1024], P('dp', 'tensor'), may hold values from -1.5 to 1.5
- branch_bias: float32 [2, 1024], replicated, may hold values from -3 to 3
- up_weight: bfloat16 [1024, 4096], P('dp', 'tensor'), may hold values from -0.1875 to 0.1875
- up_bias: float32 [4096], P('tensor'), may hold values from -3 to 3
- down_weight: bfloat16 [1024, 4096], P('dp', 'tensor'), may hold values from -0.09375 to 0.09375
- prefix_ids: int32 [10], replicated, may hold values from 0 to 9, each once
- prefix_table: float32 [10, 1024], replicated, may hold values from -1.25 to 1.25
- encoder_weight: float32 [1024, 512], P('dp'), may hold values from -0.625 to 0.625
- encoder_bias: float32 [512], replicated, may hold values from -0.625 to 0.625
- decoder_weight: float32 [512, 2, 1024], P('dp', None, 'tensor'), may hold values from -0.625 to 0.625
- decoder_bias: float32 [2, 1024], P(None, 'tensor'), may hold values from -0.625 to 0.625
- first_table: float32 [10, 1024], replicated, may hold values from -1.9073486e-06 to 1.9073486e-06
- second_table: float32 [10, 1024], replicated, may hold values from 5.3138434e-15 to 8.5369944e-14
- first_encoder: float32 [1024, 512], P('dp'), may hold values from -5.9604645e-07 to 5.9604645e-07
- second_encoder: float32 [1024, 512], P('dp'), may hold values from 3.8329363e-16 to 6.0978533e-15
- first_encoder_bias: float32 [512], replicated, may hold values from -3.33786e-06 to 3.33786e-06
- second_encoder_bias: float32 [512], replicated, may hold values from 1.0540575e-14 to 1.6899766e-13
- first_decoder: float32 [512, 2, 1024], P('dp', None, 'tensor'), may hold values from -4.7683716e-07 to 4.7683716e-07
- second_decoder: float32 [512, 2, 1024], P('dp', None, 'tensor'), may hold values from 2.230072e-16 to 3.5716e-15
- first_decoder_bias: float32 [2, 1024], P(None, 'tensor'), may hold values from -9.536743e-07 to 9.536743e-07
- second_decoder_bias: float32 [2, 1024], P(None, 'tensor'), may hold values from 8.885443e-16 to 1.42864e-14
Outputs:
- output: bfloat16 [8192, 1024], P(('dp', 'tensor'))
- input_grad: bfloat16 [8192, 1024], P(('dp', 'tensor'))
- grad_norm: float32 [], replicated
- new_table: float32 [10, 1024], replicated
- new_first_table: float32 [10, 1024], replicated
- new_second_table: float32 [10, 1024], replicated
- new_encoder: float32 [1024, 512], P('dp')
- new_first_encoder: float32 [1024, 512], P('dp')
- new_second_encoder: float32 [1024, 512], P('dp')
- new_encoder_bias: float32 [512], replicated
- new_first_encoder_bias: float32 [512], replicated
- new_second_encoder_bias: float32 [512], replicated
- new_decoder: float32 [512, 2, 1024], P('dp', None, 'tensor')
- new_first_decoder: float32 [512, 2, 1024], P('dp', None, 'tensor')
- new_second_decoder: float32 [512, 2, 1024], P('dp', None, 'tensor')
- new_decoder_bias: float32 [2, 1024], P(None, 'tensor')
- new_first_decoder_bias: float32 [2, 1024], P(None, 'tensor')
- new_second_decoder_bias: float32 [2, 1024], P(None, 'tensor')
Inputs may be any that keep to these rules, and one draw needn't show every extreme that they name: `prefix_ids`: every table row is used by exactly one prefix position.
All inputs are finite; a program needn't handle non-finite values.
Results may differ from a plain program's by a relative error of at most 0.017.
Values may be sent and summed in bfloat16 or wider, within the bound.
No kernel may reach another device: no remote copies, remote signals or barrier semaphores. Data moves between devices by JAX's collectives and lax.ppermute only.
A program may use at most 128 MiB of HBM per device.

v0:
```python
import jax
import jax.numpy as jnp
from jax import lax
from jax.sharding import PartitionSpec as P

HD = 64
PRE = 10
SEQ = 1024
STEP = 10


NORM_EPS = 1e-05
CLIP_LIMIT = 0.001
LEARN_RATE = 0.05
WEIGHT_DECAY = 0.01
BETA_FIRST = 0.9
BETA_SECOND = 0.999
ADAM_EPS = 1e-08
MASKED = -1e30
GELU_COEF = 0.7978845608028654


def layer_norm(rows, gain, shift):
    center = jnp.mean(rows, axis=-1, keepdims=True)
    offsets = rows - center
    spread = jnp.mean(offsets * offsets, axis=-1, keepdims=True)
    return offsets * lax.rsqrt(spread + NORM_EPS) * gain + shift


def norm_back(rows, gain, shift, grad_rows):
    _, pull_back = jax.vjp(lambda values: layer_norm(values, gain, shift), rows)
    return pull_back(grad_rows)[0]


def gelu_tanh(values):
    return (
        0.5 * values * (1.0 + jnp.tanh(GELU_COEF * (values + 0.044715 * values * values * values)))
    )


def adam_update(weight, grad, first, second, factor):
    clipped = grad * factor
    new_first = BETA_FIRST * first + (1.0 - BETA_FIRST) * clipped
    new_second = BETA_SECOND * second + (1.0 - BETA_SECOND) * clipped * clipped
    fix_first = 1.0 - BETA_FIRST**STEP
    fix_second = 1.0 - BETA_SECOND**STEP
    new_weight = weight * (1.0 - LEARN_RATE * WEIGHT_DECAY) - LEARN_RATE * (
        new_first / fix_first
    ) / (jnp.sqrt(new_second / fix_second) + ADAM_EPS)
    return (new_weight, new_first, new_second)


def score_blocks(query_rows, keys, prefix_keys, offset, finish, score_scale):
    pre_scores = (
        jnp.einsum("qhe,jhe->hqj", query_rows, prefix_keys, preferred_element_type=jnp.float32)
        * score_scale
    )
    own_scores = (
        jnp.einsum("qhe,khe->hqk", query_rows, keys[:finish], preferred_element_type=jnp.float32)
        * score_scale
    )
    visible = (offset + jnp.arange(finish - offset))[:, None] >= jnp.arange(finish)[None, :]
    own_scores = jnp.where(visible[None], own_scores, MASKED)
    return (pre_scores, own_scores)


def attend_forward(queries, keys, values, prefix_keys, prefix_values):
    length = queries.shape[0]
    block_rows = min(512, length)
    score_scale = float(queries.shape[2]) ** (-0.5)
    mixtures = []
    log_sums = []
    for offset in range(0, length, block_rows):
        finish = offset + block_rows
        pre_scores, own_scores = score_blocks(
            queries[offset:finish], keys, prefix_keys, offset, finish, score_scale
        )
        highest = jnp.maximum(jnp.max(pre_scores, -1), jnp.max(own_scores, -1))
        pre_exp = jnp.exp(pre_scores - highest[..., None])
        own_exp = jnp.exp(own_scores - highest[..., None])
        totals = jnp.sum(pre_exp, -1) + jnp.sum(own_exp, -1)
        pre_prob = (pre_exp / totals[..., None]).astype(jnp.bfloat16)
        own_prob = (own_exp / totals[..., None]).astype(jnp.bfloat16)
        mixture = jnp.einsum(
            "hqj,jhe->qhe", pre_prob, prefix_values, preferred_element_type=jnp.float32
        )
        mixture = mixture + jnp.einsum(
            "hqk,khe->qhe", own_prob, values[:finish], preferred_element_type=jnp.float32
        )
        mixtures.append(mixture)
        log_sums.append(highest + jnp.log(totals))
    return (jnp.concatenate(mixtures, 0), jnp.concatenate(log_sums, 1))


def attend_backward(queries, keys, values, prefix_keys, prefix_values, grad_out, log_sums):
    length = queries.shape[0]
    block_rows = min(512, length)
    score_scale = float(queries.shape[2]) ** (-0.5)
    grad_queries = []
    grad_keys = jnp.zeros(keys.shape, jnp.float32)
    grad_values = jnp.zeros(values.shape, jnp.float32)
    grad_pre_keys = jnp.zeros(prefix_keys.shape, jnp.float32)
    grad_pre_values = jnp.zeros(prefix_values.shape, jnp.float32)
    for offset in range(0, length, block_rows):
        finish = offset + block_rows
        query_rows = queries[offset:finish]
        grad_rows = grad_out[offset:finish]
        pre_scores, own_scores = score_blocks(
            query_rows, keys, prefix_keys, offset, finish, score_scale
        )
        block_sums = log_sums[:, offset:finish, None]
        pre_prob = jnp.exp(pre_scores - block_sums)
        own_prob = jnp.exp(own_scores - block_sums)
        pre_dprob = jnp.einsum(
            "qhe,jhe->hqj", grad_rows, prefix_values, preferred_element_type=jnp.float32
        )
        own_dprob = jnp.einsum(
            "qhe,khe->hqk", grad_rows, values[:finish], preferred_element_type=jnp.float32
        )
        inner = jnp.sum(pre_prob * pre_dprob, -1) + jnp.sum(own_prob * own_dprob, -1)
        pre_dscore = (pre_prob * (pre_dprob - inner[..., None])).astype(jnp.bfloat16)
        own_dscore = (own_prob * (own_dprob - inner[..., None])).astype(jnp.bfloat16)
        grad_query = jnp.einsum(
            "hqj,jhe->qhe", pre_dscore, prefix_keys, preferred_element_type=jnp.float32
        )
        grad_query = grad_query + jnp.einsum(
            "hqk,khe->qhe", own_dscore, keys[:finish], preferred_element_type=jnp.float32
        )
        grad_queries.append(grad_query * score_scale)
        grad_keys = grad_keys.at[:finish].add(
            jnp.einsum("hqk,qhe->khe", own_dscore, query_rows, preferred_element_type=jnp.float32)
            * score_scale
        )
        grad_values = grad_values.at[:finish].add(
            jnp.einsum(
                "hqk,qhe->khe",
                own_prob.astype(jnp.bfloat16),
                grad_rows,
                preferred_element_type=jnp.float32,
            )
        )
        grad_pre_keys = (
            grad_pre_keys
            + jnp.einsum("hqj,qhe->jhe", pre_dscore, query_rows, preferred_element_type=jnp.float32)
            * score_scale
        )
        grad_pre_values = grad_pre_values + jnp.einsum(
            "hqj,qhe->jhe",
            pre_prob.astype(jnp.bfloat16),
            grad_rows,
            preferred_element_type=jnp.float32,
        )
    grad_seq = jnp.stack([jnp.concatenate(grad_queries, 0), grad_keys, grad_values], 1)
    grad_prefix = jnp.stack([grad_pre_keys, grad_pre_values], 1)
    return (grad_seq, grad_prefix)


def on_device(
    tokens,
    cotangent,
    norm_params,
    attention_weight,
    attention_bias,
    merge_weight,
    branch_bias,
    up_weight,
    up_bias,
    down_weight,
    prefix_ids,
    prefix_table,
    encoder_weight,
    encoder_bias,
    decoder_weight,
    decoder_bias,
    first_table,
    second_table,
    first_encoder,
    second_encoder,
    first_encoder_bias,
    second_encoder_bias,
    first_decoder,
    second_decoder,
    first_decoder_bias,
    second_decoder_bias,
):
    highest_prec = lax.Precision.HIGHEST
    dp_index = lax.axis_index("dp")
    tok_rows = tokens.shape[0]
    local_width = merge_weight.shape[1]
    local_heads = local_width // HD
    sequences = tok_rows // SEQ
    share = tok_rows // lax.axis_size("tensor")
    row_start = lax.axis_index("tensor") * share
    gathered = (
        lax.all_gather(attention_weight, "dp", axis=0, tiled=True),
        lax.all_gather(merge_weight, "dp", axis=0, tiled=True),
        lax.all_gather(up_weight, "dp", axis=0, tiled=True),
        lax.all_gather(down_weight, "dp", axis=0, tiled=True),
        lax.all_gather(encoder_weight.astype(jnp.bfloat16), "dp", axis=0, tiled=True),
        lax.all_gather(decoder_weight.astype(jnp.bfloat16), "dp", axis=0, tiled=True),
    )
    attend_full, merge_full, up_full, down_full, encoder_full, decoder_full = gathered
    onehot = (prefix_ids[:, None] == jnp.arange(PRE, dtype=jnp.int32)[None, :]).astype(jnp.float32)
    selected = jnp.dot(onehot, prefix_table, precision=highest_prec)
    selected_low = selected.astype(jnp.bfloat16)
    encoded = jnp.dot(selected_low, encoder_full, preferred_element_type=jnp.float32) + encoder_bias
    hidden_prefix = jnp.tanh(encoded)
    hidden_low = hidden_prefix.astype(jnp.bfloat16)
    prefix_kv = (
        jnp.einsum("jp,pcm->jcm", hidden_low, decoder_full, preferred_element_type=jnp.float32)
        + decoder_bias[None]
    )
    prefix_kv = prefix_kv.astype(jnp.bfloat16).reshape(PRE, 2, local_heads, HD)
    prefix_keys = prefix_kv[:, 0]
    prefix_values = prefix_kv[:, 1]
    inputs = tokens.astype(jnp.float32)

    def forward_sequence(seq_rows):
        return attend_forward(
            seq_rows[:, 0], seq_rows[:, 1], seq_rows[:, 2], prefix_keys, prefix_values
        )

    def front(attend_mat, merge_mat, up_mat):
        normed_one = layer_norm(inputs, norm_params[0], norm_params[1]).astype(jnp.bfloat16)
        projected = (
            jnp.einsum("td,dcm->tcm", normed_one, attend_mat, preferred_element_type=jnp.float32)
            + attention_bias[None]
        )
        projected = projected.astype(jnp.bfloat16).reshape(sequences, SEQ, 3, local_heads, HD)
        mixtures, log_sums = lax.map(forward_sequence, projected)
        mixture = mixtures.reshape(tok_rows, local_width).astype(jnp.bfloat16)
        merged_part = jnp.einsum(
            "tm,dm->td", mixture, merge_mat, preferred_element_type=jnp.float32
        )
        merged = lax.psum(merged_part.astype(jnp.bfloat16), "tensor").astype(jnp.float32)
        resid = inputs + merged + branch_bias[0]
        normed_two = layer_norm(resid, norm_params[2], norm_params[3]).astype(jnp.bfloat16)
        hidden_pre = jnp.dot(normed_two, up_mat, preferred_element_type=jnp.float32) + up_bias
        return (projected, log_sums, resid, hidden_pre)

    projected, log_sums, resid, hidden_pre = front(attend_full, merge_full, up_full)
    hidden_act = gelu_tanh(hidden_pre).astype(jnp.bfloat16)
    branch_part = jnp.einsum("tf,df->td", hidden_act, down_full, preferred_element_type=jnp.float32)
    branch_out = lax.psum(branch_part.astype(jnp.bfloat16), "tensor").astype(jnp.float32)
    output_rows = (
        lax.dynamic_slice_in_dim(resid, row_start, share, 0)
        + lax.dynamic_slice_in_dim(branch_out, row_start, share, 0)
        + branch_bias[1]
    )
    regathered = (
        lax.all_gather(attention_weight, "dp", axis=0, tiled=True),
        lax.all_gather(merge_weight, "dp", axis=0, tiled=True),
        lax.all_gather(up_weight, "dp", axis=0, tiled=True),
        lax.all_gather(down_weight, "dp", axis=0, tiled=True),
        lax.all_gather(encoder_weight.astype(jnp.bfloat16), "dp", axis=0, tiled=True),
        lax.all_gather(decoder_weight.astype(jnp.bfloat16), "dp", axis=0, tiled=True),
    )
    attend_back, merge_back, up_back, down_back, encoder_back, decoder_back = regathered
    projected, log_sums, resid, hidden_pre = front(attend_back, merge_back, up_back)
    grad_hidden = jnp.dot(cotangent, down_back, preferred_element_type=jnp.float32)
    _, gelu_pull = jax.vjp(gelu_tanh, hidden_pre)
    grad_pre = gelu_pull(grad_hidden)[0].astype(jnp.bfloat16)
    up_part = jnp.einsum("tf,df->td", grad_pre, up_back, preferred_element_type=jnp.float32)
    grad_output = cotangent.astype(jnp.float32)
    up_total = lax.psum(up_part.astype(jnp.bfloat16), "tensor").astype(jnp.float32)
    grad_resid = grad_output + norm_back(resid, norm_params[2], norm_params[3], up_total)
    branch_grad = grad_resid.astype(jnp.bfloat16)
    grad_mixture = jnp.dot(branch_grad, merge_back, preferred_element_type=jnp.float32).astype(
        jnp.bfloat16
    )
    grad_mixture = grad_mixture.reshape(sequences, SEQ, local_heads, HD)

    def backward_sequence(items):
        seq_rows, grad_rows, seq_sums = items
        return attend_backward(
            seq_rows[:, 0],
            seq_rows[:, 1],
            seq_rows[:, 2],
            prefix_keys,
            prefix_values,
            grad_rows,
            seq_sums,
        )

    grad_seqs, grad_prefixes = lax.map(backward_sequence, (projected, grad_mixture, log_sums))
    grad_projected = grad_seqs.reshape(tok_rows, 3, local_width).astype(jnp.bfloat16)
    first_part = jnp.einsum(
        "tcm,dcm->td", grad_projected, attend_back, preferred_element_type=jnp.float32
    )
    first_total = lax.psum(first_part.astype(jnp.bfloat16), "tensor").astype(jnp.float32)
    input_full = grad_resid + norm_back(inputs, norm_params[0], norm_params[1], first_total)
    input_grad = lax.dynamic_slice_in_dim(input_full, row_start, share, 0)
    prefix_grad = jnp.sum(grad_prefixes, 0).reshape(PRE, 2, local_width)
    prefix_total = lax.psum(prefix_grad, "dp")
    prefix_low = prefix_total.astype(jnp.bfloat16)
    grad_decoder = jnp.einsum(
        "jp,jcm->pcm", hidden_low, prefix_low, preferred_element_type=jnp.float32
    )
    grad_decoder_bias = jnp.sum(prefix_low.astype(jnp.float32), 0)
    encoded_part = jnp.einsum(
        "jcm,pcm->jp", prefix_low, decoder_back, preferred_element_type=jnp.float32
    )
    square_part = jnp.sum(grad_decoder * grad_decoder) + jnp.sum(
        grad_decoder_bias * grad_decoder_bias
    )
    encoded_grad, square_decoder = lax.psum((encoded_part, square_part), "tensor")
    grad_encoded = (encoded_grad * (1.0 - hidden_prefix * hidden_prefix)).astype(jnp.bfloat16)
    grad_encoder = jnp.dot(selected_low.T, grad_encoded, preferred_element_type=jnp.float32)
    grad_encoder_bias = jnp.sum(grad_encoded.astype(jnp.float32), 0)
    grad_selected = jnp.dot(grad_encoded, encoder_back.T, preferred_element_type=jnp.float32)
    grad_table = jnp.dot(onehot.T, grad_selected, precision=highest_prec)
    squares = (
        square_decoder
        + jnp.sum(grad_table * grad_table)
        + jnp.sum(grad_encoder * grad_encoder)
        + jnp.sum(grad_encoder_bias * grad_encoder_bias)
    )
    grad_norm = jnp.sqrt(squares)
    factor = CLIP_LIMIT / (grad_norm + 1e-06)
    encoder_rows = encoder_weight.shape[0]
    decoder_rows = decoder_weight.shape[0]
    encoder_own = lax.dynamic_slice_in_dim(grad_encoder, dp_index * encoder_rows, encoder_rows, 0)
    decoder_own = lax.dynamic_slice_in_dim(grad_decoder, dp_index * decoder_rows, decoder_rows, 0)
    table_new = adam_update(prefix_table, grad_table, first_table, second_table, factor)
    encoder_new = adam_update(encoder_weight, encoder_own, first_encoder, second_encoder, factor)
    enc_bias_new = adam_update(
        encoder_bias, grad_encoder_bias, first_encoder_bias, second_encoder_bias, factor
    )
    decoder_new = adam_update(decoder_weight, decoder_own, first_decoder, second_decoder, factor)
    dec_bias_new = adam_update(
        decoder_bias, grad_decoder_bias, first_decoder_bias, second_decoder_bias, factor
    )
    return (
        output_rows.astype(jnp.bfloat16),
        input_grad.astype(jnp.bfloat16),
        grad_norm,
        table_new[0],
        table_new[1],
        table_new[2],
        encoder_new[0],
        encoder_new[1],
        encoder_new[2],
        enc_bias_new[0],
        enc_bias_new[1],
        enc_bias_new[2],
        decoder_new[0],
        decoder_new[1],
        decoder_new[2],
        dec_bias_new[0],
        dec_bias_new[1],
        dec_bias_new[2],
    )


def solution(mesh):
    in_specs = (
        P("dp", None),
        P("dp", None),
        P(),
        P("dp", None, "tensor"),
        P(None, "tensor"),
        P("dp", "tensor"),
        P(),
        P("dp", "tensor"),
        P("tensor"),
        P("dp", "tensor"),
        P(),
        P(),
        P("dp", None),
        P(),
        P("dp", None, "tensor"),
        P(None, "tensor"),
        P(),
        P(),
        P("dp", None),
        P("dp", None),
        P(),
        P(),
        P("dp", None, "tensor"),
        P("dp", None, "tensor"),
        P(None, "tensor"),
        P(None, "tensor"),
    )
    out_specs = (
        P(("dp", "tensor"), None),
        P(("dp", "tensor"), None),
        P(),
        P(),
        P(),
        P(),
        P("dp", None),
        P("dp", None),
        P("dp", None),
        P(),
        P(),
        P(),
        P("dp", None, "tensor"),
        P("dp", None, "tensor"),
        P("dp", None, "tensor"),
        P(None, "tensor"),
        P(None, "tensor"),
        P(None, "tensor"),
    )
    return jax.shard_map(
        on_device, mesh=mesh, in_specs=in_specs, out_specs=out_specs, check_vma=False
    )
```

profile of v0, /device:TPU:0, one launch (start us, length us, event | category | flops | bytes accessed | tf_op | source)
XLA Modules:
  0.0 531.0 jit_solution(5144852693320282007)
XLA Ops:
  15.7 34.4 %all_gather.25 = bf16[512,2,256]{2,0,1:T(8,128)(2,1)S(1)} all-gather(bf16[64,2,256]{2,0,1:T(8,128)(2,1)S(1)} %copy.110), channel_id=1, replica_groups=mesh['dp'=8,'tensor'=4] {'dp'}, dimensions={0}, use_global_device_ids=true | all-gather | bytes 589824 | tf_op jit(solution)/shard_map/all_gather | solution.py:200
  50.1 31.8 %all_gather.27 = bf16[1024,256]{1,0:T(8,128)(2,1)S(1)} all-gather(bf16[128,256]{1,0:T(8,128)(2,1)S(1)} %copy-done.46), channel_id=1, replica_groups=mesh['dp'=8,'tensor'=4] {'dp'}, dimensions={0}, use_global_device_ids=true | all-gather | bytes 589824 | tf_op jit(solution)/shard_map/all_gather | solution.py:196
  85.5 17.9 %all-gather.7.cloned.1.call-done = bf16[1024,3,256]{0,2,1:T(8,128)(2,1)} async-done(((bf16[128,3,256]{0,2,1:T(8,128)(2,1)}), bf16[1024,3,256]{0,2,1:T(8,128)(2,1)}) %all-gather.7.cloned.1.call-update) | async-done | bytes 1572880 | tf_op jit(solution)/shard_map/all_gather | solution.py:195
  103.4 3.4 add_convert_fusion.1
  116.1 2.5 fusion.21
  123.5 47.5 %all-reduce.8.cloned.1.call-done = bf16[1024,1024]{1,0:T(8,128)(2,1)} async-done(((bf16[1024,1024]{1,0:T(8,128)(2,1)}), bf16[1024,1024]{1,0:T(8,128)(2,1)}) %all-reduce.8.cloned.1.call-update) | async-done | bytes 2097168 | tf_op jit(solution)/shard_map/psum | solution.py:235
  175.8 46.3 %all-gather.9.cloned.1.call-done = bf16[1024,1024]{1,0:T(8,128)(2,1)} async-done(((bf16[128,1024]{1,0:T(8,128)(2,1)}), bf16[1024,1024]{1,0:T(8,128)(2,1)}) %all-gather.9.cloned.1.call-update) | async-done | bytes 2097168 | tf_op jit(solution)/shard_map/all_gather | solution.py:197
  222.2 7.2 %fusion.26 = f32[1024,1024]{1,0:T(8,128)} fusion(bf16[1024,1024]{1,0:T(8,128)(2,1)} %all-gather.9.cloned.1.call-done, f32[1024,1024]{1,0:T(8,128)} %copy-done.1, f32[1024]{0:T(1024)S(1)} %bitcast.198, f32[1024]{0:T(1024)S(1)} %bitcast.189, f32[1024]{0:T(1024)S(1)} %fusion.124, f32[1024]{0:T(1024)S(1)} %broadcast_multiply_fusion), kind=kOutput, calls=%fused_computation.54 | convolution fusion | flops 2152726528 | bytes 10502144 | tf_op jit(solution)/shard_map/dot_general | solution.py:238
  229.4 42.4 %all-gather.11.cloned.1.call-done = bf16[1024,1024]{1,0:T(8,128)(2,1)} async-done(((bf16[128,1024]{1,0:T(8,128)(2,1)}), bf16[1024,1024]{1,0:T(8,128)(2,1)}) %all-gather.11.cloned.1.call-update) | async-done | bytes 2097168 | tf_op jit(solution)/shard_map/all_gather | solution.py:198
  271.8 10.8 %fusion.45 = bf16[1024,1024]{1,0:T(8,128)(2,1)} fusion(bf16[1024,1024]{1,0:T(8,128)(2,1)} %all-gather.9.cloned.1.call-done, f32[1024,1024]{1,0:T(8,128)} %fusion.26, f32[1024]{0:T(1024)S(1)} %copy-done.62, bf16[1024,1024]{1,0:T(8,128)(2,1)} %param.39, bf16[1024,1024]{1,0:T(8,128)(2,1)} %all-gather.11.cloned.1.call-done), kind=kOutput, calls=%fused_computation.73 | convolution fusion | flops 4322230272 | bytes 12587008 | tf_op jit(solution)/shard_map/tf,df->td/dot_general | solution.py:263
  282.7 7.0 %fusion.48 = bf16[1024,1024]{1,0:T(8,128)(2,1)} fusion(bf16[1024,1024]{1,0:T(8,128)(2,1)} %all-gather.11.cloned.1.call-done, f32[1024,1024]{1,0:T(8,128)} %fusion.26, f32[1024]{0:T(1024)S(1)} %copy-done.62), kind=kOutput, calls=%fused_computation.74 | convolution fusion | flops 2159017984 | bytes 8392704 | tf_op jit(solution)/shard_map/tf,df->td/dot_general | solution.py:243
  289.7 43.0 %all-reduce.10.cloned.1.call-done = bf16[1024,1024]{1,0:T(8,128)(2,1)} async-done(((bf16[1024,1024]{1,0:T(8,128)(2,1)}), bf16[1024,1024]{1,0:T(8,128)(2,1)}) %all-reduce.10.cloned.1.call-update) | async-done | bytes 2097168 | tf_op jit(solution)/shard_map/psum | solution.py:265
  332.7 3.8 multiply_reduce_fusion.2
  352.2 4.9 multiply_reduce_fusion
  361.9 37.4 %psum.56 = bf16[10,2,256]{2,0,1:T(8,128)(2,1)S(1)} all-reduce(f32[10,2,256]{2,0,1:T(8,128)S(1)} %pad_maximum_fusion.2), channel_id=1, replica_groups=mesh['dp'=8,'tensor'=4] {'dp'}, use_global_device_ids=true, to_apply=%region_24.25 | all-reduce | flops 5120 | bytes 30720 | tf_op jit(solution)/shard_map/psum | solution.py:294
  403.2 5.0 fusion.64
  410.1 6.8 %multiply_convert_fusion = bf16[4,512,1024]{2,1,0:T(8,128)(2,1)S(1)} fusion(f32[4,512,1024]{2,1,0:T(8,128)} %get-tuple-element.245, f32[4,512,1024]{2,1,0:T(8,128)} %copy-done, f32[4,512]{1,0:T(4,128)S(1)} %add.428, f32[4,512]{1,0:T(4,128)S(1)} %copy-done.27), kind=kLoop, calls=%fused_computation | loop fusion | flops 8388608 | bytes 20987904 | tf_op jit(solution)/shard_map/while/body/eval_jaxpr/convert_element_type | solution.py:122
  422.4 3.8 fusion.84
  427.7 4.9 bitcast_convert_fusion
  432.6 14.0 %all-reduce.2 = (f32[]{:T(128)}, f32[10,512]{1,0:T(8,128)}) all-reduce(f32[]{:T(128)S(6)} %add.438, f32[10,512]{1,0:T(8,128)} %convolution_bitcast_fusion), channel_id=1, replica_groups=mesh['dp'=8,'tensor'=4] {'tensor'}, use_global_device_ids=true, to_apply=%region_28.29 | all-reduce | flops 5121 | bytes 40968 | tf_op jit(solution)/shard_map/psum | solution.py:306
  451.3 2.4 multiply_reduce_fusion.4
  466.1 49.0 %all-reduce.12.cloned.1.call-done = (bf16[1024,1024]{1,0:T(8,128)(2,1)}, bf16[1024,1024]{1,0:T(8,128)(2,1)}) async-done(((bf16[1024,1024]{1,0:T(8,128)(2,1)}, bf16[1024,1024]{1,0:T(8,128)(2,1)}), (bf16[1024,1024]{1,0:T(8,128)(2,1)}, bf16[1024,1024]{1,0:T(8,128)(2,1)})) %all-reduce.12.cloned.1.call-update) | async-done | bytes 4194320 | tf_op jit(solution)/shard_map/psum | solution.py:244
  515.1 2.7 fusion.14
  519.9 2.9 fusion.90
  (237 shorter events, 78.8 us)
Async XLA Ops:
  7.2 42.8 %copy-start.46 = (bf16[128,256]{1,0:T(8,128)(2,1)S(1)}, bf16[128,256]{1,0:T(8,128)(2,1)}, u32[]{:S(2)}) copy-start(bf16[128,256]{1,0:T(8,128)(2,1)} %param.43) | copy-start | bytes 196612
  7.2 75.8 %copy-start.58 = (f32[512]{0:T(512)S(1)}, f32[512]{0:T(512)}, u32[]{:S(2)}) copy-start(f32[512]{0:T(512)} %param.51) | copy-start | bytes 6148
  7.3 75.8 %all-gather.5.cloned.1.call-start = ((), (), s32[]{:S(2)}) async-start(), calls=%async_computation | async-start | bytes 1179648 | tf_op jit(solution)/shard_map/all_gather | solution.py:199
  9.1 76.1 %copy-start.57 = (f32[2,256]{1,0:T(2,128)S(1)}, f32[2,256]{1,0:T(2,128)}, u32[]{:S(2)}) copy-start(f32[2,256]{1,0:T(2,128)} %param.53) | copy-start | bytes 6148
  9.1 94.3 %all-gather.7.cloned.1.call-start = ((), (), s32[]{:S(2)}) async-start(), calls=%async_computation.1 | async-start | bytes 1769472 | tf_op jit(solution)/shard_map/all_gather | solution.py:195
  10.9 92.5 %copy-start.61 = (f32[3,256]{1,0:T(4,128)S(1)}, f32[3,256]{1,0:T(4,128)}, u32[]{:S(2)}) copy-start(f32[3,256]{1,0:T(4,128)} %param.42) | copy-start | bytes 9220
  10.9 160.1 %all-reduce.8.cloned.1.call-start = ((), (), s32[]{:S(2)}) async-start(), calls=%async_computation.2 | async-start | bytes 4194304 | tf_op jit(solution)/shard_map/psum | solution.py:235
  14.6 92.2 %copy-start.44 = (f32[1024]{0:T(1024)}, f32[1024]{0:T(1024)S(1)}, u32[]{:S(2)}) copy-start(f32[1024]{0:T(1024)S(1)} %broadcast_multiply_fusion.1) | copy-start | bytes 12292
  15.3 66.6 %copy-start.49 = (f32[1024]{0:T(1024)}, f32[1024]{0:T(1024)S(1)}, u32[]{:S(2)}) copy-start(f32[1024]{0:T(1024)S(1)} %fusion.10) | copy-start | bytes 12292
  15.4 91.5 %copy-start.53 = (f32[1024]{0:T(1024)}, f32[1024]{0:T(1024)S(1)}, u32[]{:S(2)}) copy-start(f32[1024]{0:T(1024)S(1)} %fusion.123) | copy-start | bytes 12292
  15.4 91.4 %copy-start.47 = (f32[1,1024]{1,0:T(1,128)}, f32[1,1024]{1,0:T(1,128)S(1)}, u32[]{:S(2)}) copy-start(f32[1,1024]{1,0:T(1,128)S(1)} %get-tuple-element.230) | copy-start | bytes 12292
  15.6 91.2 %copy-start.30 = (bf16[10,1024]{1,0:T(8,128)(2,1)}, bf16[10,1024]{1,0:T(8,128)(2,1)S(1)}, u32[]{:S(2)}) copy-start(bf16[10,1024]{1,0:T(8,128)(2,1)S(1)} %convolution_convert_fusion.1) | copy-start | bytes 61444
  121.3 100.9 %all-gather.9.cloned.1.call-start = ((), (), s32[]{:S(2)}) async-start(), calls=%async_computation.3 | async-start | bytes 2359296 | tf_op jit(solution)/shard_map/all_gather | solution.py:197
  121.9 149.9 %all-gather.11.cloned.1.call-start = ((), (), s32[]{:S(2)}) async-start(), calls=%async_computation.4 | async-start | bytes 2359296 | tf_op jit(solution)/shard_map/all_gather | solution.py:198
  122.5 210.2 %all-reduce.10.cloned.1.call-start = ((), (), s32[]{:S(2)}) async-start(), calls=%async_computation.5 | async-start | bytes 4194304 | tf_op jit(solution)/shard_map/psum | solution.py:265
  222.2 49.6 %copy-start.62 = (f32[1024]{0:T(1024)S(1)}, f32[1024]{0:T(1024)}, u32[]{:S(2)}) copy-start(f32[1024]{0:T(1024)} %param.46) | copy-start | bytes 12292
  282.6 232.5 %all-reduce.12.cloned.1.call-start = ((), (), s32[]{:S(2)}) async-start(), calls=%async_computation.6 | async-start | bytes 8388608 | tf_op jit(solution)/shard_map/psum | solution.py:244
  352.2 48.0 %copy-start.40 = (bf16[10,1,4,64]{3,2,0,1:T(4,128)(2,1)S(1)}, bf16[10,1,4,64]{3,2,0,1:T(4,128)(2,1)}, u32[]{:S(2)}) copy-start(bf16[10,1,4,64]{3,2,0,1:T(4,128)(2,1)} %copy-done.39) | copy-start | bytes 15364
  352.2 49.1 %copy-start.23 = (f32[10,512]{1,0:T(8,128)S(1)}, f32[10,512]{1,0:T(8,128)}, u32[]{:S(2)}) copy-start(f32[10,512]{1,0:T(8,128)} %copy-done.22) | copy-start | bytes 61444
  357.1 46.1 %copy-start.27 = (f32[4,512]{1,0:T(4,128)S(1)}, f32[4,512]{1,0:T(4,128)}, u32[]{:S(2)}) copy-start(f32[4,512]{1,0:T(4,128)} %get-tuple-element.220) | copy-start | bytes 24580
  453.8 64.1 %copy-start.50 = (f32[1024]{0:T(1024)S(1)}, f32[1024]{0:T(1024)}, u32[]{:S(2)}) copy-start(f32[1024]{0:T(1024)} %copy-done.49) | copy-start | bytes 12292
  453.8 64.1 %copy-start.45 = (f32[1024]{0:T(1024)S(1)}, f32[1024]{0:T(1024)}, u32[]{:S(2)}) copy-start(f32[1024]{0:T(1024)} %copy-done.44) | copy-start | bytes 12292
  453.8 64.1 %copy-start.48 = (f32[1,1024]{1,0:T(1,128)S(1)}, f32[1,1024]{1,0:T(1,128)}, u32[]{:S(2)}) copy-start(f32[1,1024]{1,0:T(1,128)} %copy-done.47) | copy-start | bytes 12292
  453.8 64.1 %copy-start.54 = (f32[1024]{0:T(1024)S(1)}, f32[1024]{0:T(1024)}, u32[]{:S(2)}) copy-start(f32[1024]{0:T(1024)} %copy-done.53) | copy-start | bytes 12292
  (48 other events, 370.4 us)
Sparse Core Ops, SparseCore 0:
  10.8 46.0 all-gather.4
  59.5 43.8 all-gather.6
  121.4 49.5 all-reduce.7
  173.0 49.1 all-gather.8
  224.2 47.6 all-gather.10
  282.7 49.9 all-reduce.9
  432.8 82.3 all-reduce.11
where the time goes:
time: 540 us; the launch traced here: 531 us
  waiting for transfers between devices  247 us (46%)
  blocking collectives  118 us (22%)
  matrix products  78.6 us (15%)
  other arithmetic  49.2 us (9%)
  between operations  20.3 us (4%)
  local copies, waits for them, and re-layouts  17.3 us (3%)
    psum x1, waiting for transfers between devices, on_device(): lax.psum(branch_part.astype(jnp.bfloat16), 'tensor').astype(jnp.float32)  49 us
    psum x1, waiting for transfers between devices, front(): lax.psum(merged_part.astype(jnp.bfloat16), 'tensor').astype(jnp.float32)  47.5 us
    all_gather x1, waiting for transfers between devices, on_device(): lax.all_gather(up_weight, 'dp', axis=0, tiled=True)  46.3 us
    psum x1, waiting for transfers between devices, on_device(): lax.psum(up_part.astype(jnp.bfloat16), 'tensor').astype(jnp.float32)  43 us
    all_gather x1, waiting for transfers between devices, on_device(): lax.all_gather(down_weight, 'dp', axis=0, tiled=True)  42.4 us
    psum x1, blocking collectives, on_device(): prefix_total = lax.psum(prefix_grad, 'dp')  37.4 us
    all_gather x1, blocking collectives, on_device(): lax.all_gather(decoder_weight.astype(jnp.bfloat16), 'dp', axis=0, tiled=T...  34.4 us
    all_gather x1, blocking collectives, on_device(): lax.all_gather(merge_weight, 'dp', axis=0, tiled=True)  31.8 us
  transfers between devices with their start and end apart: 7, of which 6 were waited for; matrix products, arithmetic and copies ran while one was open for 8% of the time, Pallas kernels for 0%

commit v1 on v0

--- a/solution.py
+++ b/solution.py
@@ -1,6 +1,8 @@
 import jax
 import jax.numpy as jnp
 from jax import lax
+from jax.experimental import pallas as pl
+from jax.experimental.pallas import tpu as pltpu
 from jax.sharding import PartitionSpec as P
 
 HD = 64
@@ -153,6 +155,86 @@
     grad_seq = jnp.stack([jnp.concatenate(grad_queries, 0), grad_keys, grad_values], 1)
     grad_prefix = jnp.stack([grad_pre_keys, grad_pre_values], 1)
     return (grad_seq, grad_prefix)
+
+
+def swap(values, axis, bit):
+    size = lax.axis_size(axis)
+    return lax.ppermute(values, axis, [(i, i ^ bit) for i in range(size)])
+
+
+def assemble_kernel(own, far, near, side, side_rest, out, sems):
+    here = lax.axis_index("dp")
+    pieces = [(own, 0), (far, 4), (near.at[0], 2), (near.at[1], 6)]
+    pieces += [(side, 1), (side_rest.at[0], 5), (side_rest.at[1], 3), (side_rest.at[2], 7)]
+    copies = []
+    for slot, (piece, offset) in enumerate(pieces):
+        place = lax.bitwise_xor(here, offset)
+        copies.append(pltpu.make_async_copy(piece, out.at[place], sems.at[slot]))
+        copies[-1].start()
+    for copy in copies:
+        copy.wait()
+
+
+def gather_start(shard):
+    return swap(shard, "dp", 1), swap(shard, "dp", 4)
+
+
+def gather_rest(shard, side, far):
+    near = swap(jnp.stack([shard, far]), "dp", 2)
+    side_rest = swap(jnp.concatenate([far[None], near]), "dp", 1)
+    return near, side_rest
+
+
+def assemble(shard, far, near, side, side_rest):
+    return pl.pallas_call(
+        assemble_kernel,
+        out_shape=jax.ShapeDtypeStruct((8,) + shard.shape, shard.dtype),
+        in_specs=[pl.BlockSpec(memory_space=pl.ANY)] * 5,
+        out_specs=pl.BlockSpec(memory_space=pl.ANY),
+        scratch_shapes=[pltpu.SemaphoreType.DMA((8,))],
+    )(shard, far, near, side, side_rest)
+
+
+def gather_all(shards):
+    if lax.axis_size("dp") != 8:
+        return [lax.all_gather(shard, "dp", axis=0) for shard in shards]
+    fulls = []
+    after = None
+    for shard in shards:
+        if after is not None:
+            shard, after = lax.optimization_barrier((shard, after))
+        side, far = gather_start(shard)
+        after = far
+        near, side_rest = gather_rest(shard, side, far)
+        fulls.append(assemble(shard, far, near, side, side_rest))
+    return fulls
+
+
+def sum_over(values, axis):
+    bit = 1
+    while bit < lax.axis_size(axis):
+        values = jax.tree.map(lambda v, b=bit: v + swap(v, axis, b), values)
+        bit *= 2
+    return values
+
+
+def scatter_rows(part):
+    low = part.astype(jnp.bfloat16)
+    rows, width = part.shape
+    here = lax.axis_index("tensor")
+    core, side = here % 2, here // 2
+    blocks = low.reshape(2, 2, rows // 4, width)
+    keep = lax.dynamic_index_in_dim(blocks, core, 1, keepdims=False)
+    got = swap(lax.dynamic_index_in_dim(blocks, 1 - core, 1, keepdims=False), "tensor", 1)
+    both = keep.astype(jnp.float32) + got.astype(jnp.float32)
+    mine = lax.dynamic_index_in_dim(both, side, 0, keepdims=False)
+    other = lax.dynamic_index_in_dim(both, 1 - side, 0, keepdims=False).astype(jnp.bfloat16)
+    return mine + swap(other, "tensor", 2).astype(jnp.float32)
+
+
+def split_low(values):
+    high = lax.reduce_precision(values, 8, 7)
+    return jnp.stack([high.astype(jnp.bfloat16), (values - high).astype(jnp.bfloat16)])
 
 
 def on_device(
@@ -185,25 +267,50 @@
 ):
     highest_prec = lax.Precision.HIGHEST
     dp_index = lax.axis_index("dp")
-    tok_rows = tokens.shape[0]
+    here = lax.axis_index("tensor")
+    core, side = here % 2, here // 2
+    tok_rows, width = tokens.shape
     local_width = merge_weight.shape[1]
     local_heads = local_width // HD
     sequences = tok_rows // SEQ
     share = tok_rows // lax.axis_size("tensor")
-    row_start = lax.axis_index("tensor") * share
-    gathered = (
-        lax.all_gather(attention_weight, "dp", axis=0, tiled=True),
-        lax.all_gather(merge_weight, "dp", axis=0, tiled=True),
-        lax.all_gather(up_weight, "dp", axis=0, tiled=True),
-        lax.all_gather(down_weight, "dp", axis=0, tiled=True),
-        lax.all_gather(encoder_weight.astype(jnp.bfloat16), "dp", axis=0, tiled=True),
-        lax.all_gather(decoder_weight.astype(jnp.bfloat16), "dp", axis=0, tiled=True),
-    )
-    attend_full, merge_full, up_full, down_full, encoder_full, decoder_full = gathered
+    row_start = here * share
+    in_rows = attention_weight.shape[0]
+    encoder_rows = encoder_weight.shape[0]
+    decoder_rows = decoder_weight.shape[0]
+    hidden = encoder_weight.shape[1]
+
     onehot = (prefix_ids[:, None] == jnp.arange(PRE, dtype=jnp.int32)[None, :]).astype(jnp.float32)
     selected = jnp.dot(onehot, prefix_table, precision=highest_prec)
     selected_low = selected.astype(jnp.bfloat16)
-    encoded = jnp.dot(selected_low, encoder_full, preferred_element_type=jnp.float32) + encoder_bias
+    selected_own = lax.dynamic_slice_in_dim(
+        selected_low, dp_index * encoder_rows, encoder_rows, 1
+    )
+    encoder_low = encoder_weight.astype(jnp.bfloat16)
+    decoder_low = decoder_weight.astype(jnp.bfloat16)
+    encoded_own = jnp.dot(selected_own, encoder_low, preferred_element_type=jnp.float32)
+    sent = split_low(encoded_own).reshape(-1, local_width)
+    sent_rows = sent.shape[0]
+    sent = jnp.pad(sent, ((0, -sent_rows % 16), (0, 0)))
+    first = jnp.concatenate(
+        [attention_weight.transpose(1, 0, 2).reshape(3 * in_rows, local_width), sent]
+    )
+    second = jnp.concatenate([merge_weight, decoder_low.reshape(2 * decoder_rows, local_width)])
+    first, second, down_all, up_all, encoder_all = gather_all(
+        [first, second, down_weight, up_weight, encoder_low]
+    )
+    attend_full = first[:, : 3 * in_rows].reshape(-1, 3, in_rows, local_width)
+    attend_full = attend_full.transpose(1, 0, 2, 3).reshape(3, width, local_width)
+    encoded_all = first[:, 3 * in_rows : 3 * in_rows + sent_rows]
+    encoded = (
+        jnp.sum(encoded_all.astype(jnp.float32).reshape(-1, PRE, hidden), 0) + encoder_bias
+    )
+    merge_own = second[:, : merge_weight.shape[0]].reshape(width, local_width)
+    decoder_full = second[:, merge_weight.shape[0] :].reshape(hidden, 2, local_width)
+    down_full = down_all.reshape(width, -1)
+    up_full = up_all.reshape(width, -1)
+    encoder_full = encoder_all.reshape(width, hidden)
+
     hidden_prefix = jnp.tanh(encoded)
     hidden_low = hidden_prefix.astype(jnp.bfloat16)
     prefix_kv = (
@@ -215,99 +322,93 @@
     prefix_values = prefix_kv[:, 1]
     inputs = tokens.astype(jnp.float32)
 
-    def forward_sequence(seq_rows):
-        return attend_forward(
-            seq_rows[:, 0], seq_rows[:, 1], seq_rows[:, 2], prefix_keys, prefix_values
-        )
-
-    def front(attend_mat, merge_mat, up_mat):
-        normed_one = layer_norm(inputs, norm_params[0], norm_params[1]).astype(jnp.bfloat16)
-        projected = (
-            jnp.einsum("td,dcm->tcm", normed_one, attend_mat, preferred_element_type=jnp.float32)
-            + attention_bias[None]
-        )
-        projected = projected.astype(jnp.bfloat16).reshape(sequences, SEQ, 3, local_heads, HD)
-        mixtures, log_sums = lax.map(forward_sequence, projected)
-        mixture = mixtures.reshape(tok_rows, local_width).astype(jnp.bfloat16)
-        merged_part = jnp.einsum(
-            "tm,dm->td", mixture, merge_mat, preferred_element_type=jnp.float32
-        )
-        merged = lax.psum(merged_part.astype(jnp.bfloat16), "tensor").astype(jnp.float32)
-        resid = inputs + merged + branch_bias[0]
-        normed_two = layer_norm(resid, norm_params[2], norm_params[3]).astype(jnp.bfloat16)
-        hidden_pre = jnp.dot(normed_two, up_mat, preferred_element_type=jnp.float32) + up_bias
-        return (projected, log_sums, resid, hidden_pre)
-
-    projected, log_sums, resid, hidden_pre = front(attend_full, merge_full, up_full)
+    merge_side = swap(merge_own, "tensor", 2)
+    merge_pair = swap(jnp.stack([merge_own, merge_side]), "tensor", 1)
+
+    normed_one = layer_norm(inputs, norm_params[0], norm_params[1]).astype(jnp.bfloat16)
+    projected = (
+        jnp.einsum("td,cdm->tcm", normed_one, attend_full, preferred_element_type=jnp.float32)
+        + attention_bias[None]
+    )
+    projected = projected.astype(jnp.bfloat16).reshape(tok_rows, 3, local_heads, HD)
+    mixture, log_sums = attend_forward(
+        projected[:, 0], projected[:, 1], projected[:, 2], prefix_keys, prefix_values
+    )
+    mixture = mixture.reshape(tok_rows, local_width).astype(jnp.bfloat16)
+    mixture_side = swap(mixture, "tensor", 2)
+    mixture_pair = swap(jnp.stack([mixture, mixture_side]), "tensor", 1)
+    mixture_cat = jnp.concatenate(
+        [mixture, mixture_side, mixture_pair[0], mixture_pair[1]], 1
+    )
+    merge_cat = jnp.concatenate([merge_own, merge_side, merge_pair[0], merge_pair[1]], 1)
+    merged = jnp.einsum("tm,dm->td", mixture_cat, merge_cat, preferred_element_type=jnp.float32)
+    resid = inputs + merged + branch_bias[0]
+    normed_two = layer_norm(resid, norm_params[2], norm_params[3]).astype(jnp.bfloat16)
+    hidden_pre = jnp.dot(normed_two, up_full, preferred_element_type=jnp.float32) + up_bias
     hidden_act = gelu_tanh(hidden_pre).astype(jnp.bfloat16)
     branch_part = jnp.einsum("tf,df->td", hidden_act, down_full, preferred_element_type=jnp.float32)
-    branch_out = lax.psum(branch_part.astype(jnp.bfloat16), "tensor").astype(jnp.float32)
-    output_rows = (
-        lax.dynamic_slice_in_dim(resid, row_start, share, 0)
-        + lax.dynamic_slice_in_dim(branch_out, row_start, share, 0)
-        + branch_bias[1]
-    )
-    regathered = (
-        lax.all_gather(attention_weight, "dp", axis=0, tiled=True),
-        lax.all_gather(merge_weight, "dp", axis=0, tiled=True),
-        lax.all_gather(up_weight, "dp", axis=0, tiled=True),
-        lax.all_gather(down_weight, "dp", axis=0, tiled=True),
-        lax.all_gather(encoder_weight.astype(jnp.bfloat16), "dp", axis=0, tiled=True),
-        lax.all_gather(decoder_weight.astype(jnp.bfloat16), "dp", axis=0, tiled=True),
-    )
-    attend_back, merge_back, up_back, down_back, encoder_back, decoder_back = regathered
-    projected, log_sums, resid, hidden_pre = front(attend_back, merge_back, up_back)
-    grad_hidden = jnp.dot(cotangent, down_back, preferred_element_type=jnp.float32)
+    resid_own = lax.dynamic_slice_in_dim(resid, row_start, share, 0)
+
+    grad_hidden = jnp.dot(cotangent, down_full, preferred_element_type=jnp.float32)
     _, gelu_pull = jax.vjp(gelu_tanh, hidden_pre)
     grad_pre = gelu_pull(grad_hidden)[0].astype(jnp.bfloat16)
-    up_part = jnp.einsum("tf,df->td", grad_pre, up_back, preferred_element_type=jnp.float32)
-    grad_output = cotangent.astype(jnp.float32)
-    up_total = lax.psum(up_part.astype(jnp.bfloat16), "tensor").astype(jnp.float32)
-    grad_resid = grad_output + norm_back(resid, norm_params[2], norm_params[3], up_total)
+    up_part = jnp.einsum("tf,df->td", grad_pre, up_full, preferred_element_type=jnp.float32)
+    up_own = scatter_rows(up_part)
+    branch_own = scatter_rows(branch_part)
+    output_rows = resid_own + branch_own + branch_bias[1]
+    cotangent_own = lax.dynamic_slice_in_dim(cotangent, row_start, share, 0).astype(jnp.float32)
+    grad_resid = cotangent_own + norm_back(resid_own, norm_params[2], norm_params[3], up_own)
     branch_grad = grad_resid.astype(jnp.bfloat16)
-    grad_mixture = jnp.dot(branch_grad, merge_back, preferred_element_type=jnp.float32).astype(
-        jnp.bfloat16
-    )
-    grad_mixture = grad_mixture.reshape(sequences, SEQ, local_heads, HD)
-
-    def backward_sequence(items):
-        seq_rows, grad_rows, seq_sums = items
-        return attend_backward(
-            seq_rows[:, 0],
-            seq_rows[:, 1],
-            seq_rows[:, 2],
-            prefix_keys,
-            prefix_values,
-            grad_rows,
-            seq_sums,
-        )
-
-    grad_seqs, grad_prefixes = lax.map(backward_sequence, (projected, grad_mixture, log_sums))
-    grad_projected = grad_seqs.reshape(tok_rows, 3, local_width).astype(jnp.bfloat16)
+    grad_cat = jnp.dot(branch_grad, merge_cat, preferred_element_type=jnp.float32)
+    grad_cat = grad_cat.astype(jnp.bfloat16)
+    grad_blocks = [grad_cat[:, i * local_width : (i + 1) * local_width] for i in range(4)]
+    from_side = swap(jnp.stack([grad_blocks[1], grad_blocks[3]]), "tensor", 2)
+    from_pair = swap(jnp.stack([grad_blocks[2], from_side[1]]), "tensor", 1)
+    by_offset = jnp.stack([grad_blocks[0], from_pair[0], from_side[0], from_pair[1]])
+    order = lax.bitwise_xor(jnp.arange(4), here)
+    grad_mixture = jnp.stack(
+        [lax.dynamic_index_in_dim(by_offset, order[i], 0, keepdims=False) for i in range(4)]
+    )
+    grad_mixture = grad_mixture.reshape(tok_rows, local_heads, HD)
+
+    grad_seq, grad_prefix = attend_backward(
+        projected[:, 0],
+        projected[:, 1],
+        projected[:, 2],
+        prefix_keys,
+        prefix_values,
+        grad_mixture,
+        log_sums,
+    )
+    grad_projected = grad_seq.reshape(tok_rows, 3, local_width).astype(jnp.bfloat16)
     first_part = jnp.einsum(
-        "tcm,dcm->td", grad_projected, attend_back, preferred_element_type=jnp.float32
-    )
-    first_total = lax.psum(first_part.astype(jnp.bfloat16), "tensor").astype(jnp.float32)
-    input_full = grad_resid + norm_back(inputs, norm_params[0], norm_params[1], first_total)
-    input_grad = lax.dynamic_slice_in_dim(input_full, row_start, share, 0)
-    prefix_grad = jnp.sum(grad_prefixes, 0).reshape(PRE, 2, local_width)
-    prefix_total = lax.psum(prefix_grad, "dp")
+        "tcm,cdm->td", grad_projected, attend_full, preferred_element_type=jnp.float32
+    )
+    first_own = scatter_rows(first_part)
+    inputs_own = lax.dynamic_slice_in_dim(inputs, row_start, share, 0)
+    input_grad = grad_resid + norm_back(inputs_own, norm_params[0], norm_params[1], first_own)
+
+    prefix_total = sum_over(grad_prefix.reshape(PRE, 2, local_width), "dp")
     prefix_low = prefix_total.astype(jnp.bfloat16)
     grad_decoder = jnp.einsum(
         "jp,jcm->pcm", hidden_low, prefix_low, preferred_element_type=jnp.float32
     )
     grad_decoder_bias = jnp.sum(prefix_low.astype(jnp.float32), 0)
     encoded_part = jnp.einsum(
-        "jcm,pcm->jp", prefix_low, decoder_back, preferred_element_type=jnp.float32
+        "jcm,pcm->jp", prefix_low, decoder_full, preferred_element_type=jnp.float32
     )
     square_part = jnp.sum(grad_decoder * grad_decoder) + jnp.sum(
         grad_decoder_bias * grad_decoder_bias
     )
-    encoded_grad, square_decoder = lax.psum((encoded_part, square_part), "tensor")
+    joint = jnp.concatenate(
+        [encoded_part, jnp.broadcast_to(square_part, (1, hidden))]
+    )
+    joint = sum_over(joint, "tensor")
+    encoded_grad, square_decoder = joint[:PRE], joint[PRE, 0]
     grad_encoded = (encoded_grad * (1.0 - hidden_prefix * hidden_prefix)).astype(jnp.bfloat16)
     grad_encoder = jnp.dot(selected_low.T, grad_encoded, preferred_element_type=jnp.float32)
     grad_encoder_bias = jnp.sum(grad_encoded.astype(jnp.float32), 0)
-    grad_selected = jnp.dot(grad_encoded, encoder_back.T, preferred_element_type=jnp.float32)
+    grad_selected = jnp.dot(grad_encoded, encoder_full.T, preferred_element_type=jnp.float32)
     grad_table = jnp.dot(onehot.T, grad_selected, precision=highest_prec)
     squares = (
         square_decoder
@@ -317,8 +418,6 @@
     )
     grad_norm = jnp.sqrt(squares)
     factor = CLIP_LIMIT / (grad_norm + 1e-06)
-    encoder_rows = encoder_weight.shape[0]
-    decoder_rows = decoder_weight.shape[0]
     encoder_own = lax.dynamic_slice_in_dim(grad_encoder, dp_index * encoder_rows, encoder_rows, 0)
     decoder_own = lax.dynamic_slice_in_dim(grad_decoder, dp_index * decoder_rows, decoder_rows, 0)
     table_new = adam_update(prefix_table, grad_table, first_table, second_table, factor)

time: 540 us -> 627 us (1.16)
  Pallas kernels: 0 us -> 250 us
  waiting for transfers between devices: 247 us -> 113 us
  blocking collectives: 118 us -> 0 us
  local copies, waits for them, and re-layouts: 17.3 us -> 66.4 us
  starting transfers between devices: 0.63 us -> 39.2 us
  other arithmetic: 49.2 us -> 55.7 us
    pallas_call x0 -> x5, Pallas kernels: none -> 250 us  [assemble(): pl.pallas_call(assemble_kernel, out_shape=jax.ShapeDtypeStruct((8,) + sha...]
    psum x3 -> x0, waiting for transfers between devices: 139 us -> none  [the longest x1 49 us: on_device(): lax.psum(branch_part.astype(jnp.bfloat16), 'tensor').astype(jnp.float32)]
    ppermute x0 -> x37, waiting for transfers between devices: none -> 113 us  [swap(): return lax.ppermute(values, axis, [(i, i ^ bit) for i in range(size)])]
    all_gather x4 -> x0, waiting for transfers between devices: 107 us -> none  [the longest x1 46.3 us: on_device(): lax.all_gather(up_weight, 'dp', axis=0, tiled=True)]
    all_gather x2 -> x0, blocking collectives: 66.2 us -> none  [the longest x1 34.4 us: on_device(): lax.all_gather(decoder_weight.astype(jnp.bfloat16), 'dp', axis=0, tiled=T...]
    psum x2 -> x0, blocking collectives: 51.4 us -> none  [the longest x1 37.4 us: on_device(): prefix_total = lax.psum(prefix_grad, 'dp')]
    ppermute x0 -> x37, starting transfers between devices: none -> 39.2 us  [swap(): return lax.ppermute(values, axis, [(i, i ^ bit) for i in range(size)])]
    dynamic_slice x1 -> x7, local copies, waits for them, and re-layouts: 0.08 us -> 13.3 us  [the longest x3 6.82 us: scatter_rows(): lax.dynamic_index_in_dim(blocks, 1 - core, 1, keepdims=False)]
  transfers between devices with their start and end apart: 7 -> 37, of which waited for: 6 -> 15; matrix products, arithmetic and copies ran while one was open for 8% -> 18% of each run, Pallas kernels for 0% -> 40%
where the time goes in v1:
time: 627 us; the launch traced here: 618 us
  Pallas kernels  250 us (40%)
  waiting for transfers between devices  113 us (18%)
  matrix products  78 us (12%)
  local copies, waits for them, and re-layouts  66.4 us (11%)
  other arithmetic  55.7 us (9%)
  starting transfers between devices  39.2 us (6%)
  between operations  15.4 us (2%)
    pallas_call x5, Pallas kernels, assemble(): pl.pallas_call(assemble_kernel, out_shape=jax.ShapeDtypeStruct((8,) + sha...  250 us
    ppermute x37, waiting for transfers between devices, swap(): return lax.ppermute(values, axis, [(i, i ^ bit) for i in range(size)])  113 us
    ppermute x37, starting transfers between devices, swap(): return lax.ppermute(values, axis, [(i, i ^ bit) for i in range(size)])  39.2 us
    unnamed x175, local copies, waits for them, and re-layouts  24 us
  transfers between devices with their start and end apart: 37, of which 15 were waited for; matrix products, arithmetic and copies ran while one was open for 18% of the time, Pallas kernels for 40%

profile of v1, /device:TPU:0, one launch (start us, length us, event | category | flops | bytes accessed | tf_op | source)
XLA Modules:
  0.0 618.1 jit_solution(3203079578788420218)
XLA Ops:
  5.2 4.1 collective-permute-start
  10.8 3.9 copy.77
  19.7 4.2 collective-permute-start.1
  23.9 4.5 collective-permute-done.4.far
  31.5 15.1 %collective-permute-done.5.near = bf16[2,256,256]{2,1,0:T(8,128)(2,1)S(1)} collective-permute-done((bf16[2,256,256]{2,1,0:T(8,128)(2,1)S(1)}, bf16[2,256,256]{2,1,0:T(8,128)(2,1)S(1)}, u32[]{:S(2)}, u32[]{:S(2)}) %collective-permute-start.5) | collective-permute-done | bytes 262176 | tf_op jit(solution)/shard_map/ppermute | solution.py:162
  53.9 8.3 %collective-permute-done.13.far = bf16[128,1024]{1,0:T(8,128)(2,1)S(1)} collective-permute-done((bf16[128,1024]{1,0:T(8,128)(2,1)}, bf16[128,1024]{1,0:T(8,128)(2,1)S(1)}, u32[]{:S(2)}, u32[]{:S(2)}) %collective-permute-start.13) | collective-permute-done | bytes 262176 | tf_op jit(solution)/shard_map/ppermute | solution.py:162
  64.0 9.9 %collective-permute-done.6.side = bf16[256,256]{1,0:T(8,128)(2,1)S(1)} collective-permute-done((bf16[256,256]{1,0:T(8,128)(2,1)S(1)}, bf16[256,256]{1,0:T(8,128)(2,1)S(1)}, u32[]{:S(2)}, u32[]{:S(2)}) %collective-permute-start.6) | collective-permute-done | bytes 131104 | tf_op jit(solution)/shard_map/ppermute | solution.py:162
  74.6 32.9 %shard_map.396 = bf16[8,256,256]{2,1,0:T(8,128)(2,1)} custom-call(bf16[256,256]{1,0:T(8,128)(2,1)} %copy-done.36, bf16[256,256]{1,0:T(8,128)(2,1)} %copy-done.37, bf16[2,256,256]{2,1,0:T(8,128)(2,1)} %copy-done.41, bf16[256,256]{1,0:T(8,128)(2,1)} %copy-done.61, bf16[3,256,256]{2,1,0:T(8,128)(2,1)} %collective-permute-done.7.side_rest), custom_call_target="tpu_custom_call" | custom-call | tf_op jit(solution)/shard_map/pallas_call | solution.py:189
  112.7 54.8 %shard_map.395 = bf16[8,432,256]{2,1,0:T(8,128)(2,1)} custom-call(bf16[432,256]{1,0:T(8,128)(2,1)} %get-tuple-element.183.own, bf16[432,256]{1,0:T(8,128)(2,1)} %copy-done.34, bf16[2,432,256]{2,1,0:T(8,128)(2,1)} %copy-done.35, bf16[432,256]{1,0:T(8,128)(2,1)} %collective-permute-done.2.side, bf16[3,432,256]{2,1,0:T(8,128)(2,1)} %collective-permute-done.3.side_rest), custom_call_target="tpu_custom_call" | custom-call | tf_op jit(solution)/shard_map/pallas_call | solution.py:189
  181.6 4.2 add_convert_fusion.2
  212.7 27.9 %collective-permute-done.18.side = bf16[128,1024]{1,0:T(8,128)(2,1)S(1)} collective-permute-done((bf16[128,1024]{1,0:T(8,128)(2,1)S(1)}, bf16[128,1024]{1,0:T(8,128)(2,1)S(1)}, u32[]{:S(2)}, u32[]{:S(2)}) %collective-permute-start.18) | collective-permute-done | bytes 262176 | tf_op jit(solution)/shard_map/ppermute | solution.py:162
  242.1 64.7 %shard_map.398 = bf16[8,128,1024]{2,1,0:T(8,128)(2,1)} custom-call(bf16[128,1024]{1,0:T(8,128)(2,1)} %own.1, bf16[128,1024]{1,0:T(8,128)(2,1)} %copy-done.21, bf16[2,128,1024]{2,1,0:T(8,128)(2,1)} %collective-permute-done.17.near, bf16[128,1024]{1,0:T(8,128)(2,1)} %copy-done.56, bf16[3,128,1024]{2,1,0:T(8,128)(2,1)} %collective-permute-done.19.side_rest), custom_call_target="tpu_custom_call" | custom-call | tf_op jit(solution)/shard_map/pallas_call | solution.py:189
  306.9 64.7 %shard_map.397 = bf16[8,128,1024]{2,1,0:T(8,128)(2,1)} custom-call(bf16[128,1024]{1,0:T(8,128)(2,1)} %own, bf16[128,1024]{1,0:T(8,128)(2,1)} %copy-done.22, bf16[2,128,1024]{2,1,0:T(8,128)(2,1)} %collective-permute-done.14.near, bf16[128,1024]{1,0:T(8,128)(2,1)} %collective-permute-done.15.side, bf16[3,128,1024]{2,1,0:T(8,128)(2,1)} %collective-permute-done.16.side_rest), custom_call_target="tpu_custom_call" | custom-call | tf_op jit(solution)/shard_map/pallas_call | solution.py:189
  386.1 4.1 fusion.42
  390.2 11.3 %convolution_convert_fusion = bf16[1024,1024]{1,0:T(8,128)(2,1)} fusion(bf16[1024,1024]{1,0:T(8,128)(2,1)} %bitcast.304, f32[1024,1024]{1,0:T(8,128)} %copy-done.77, bf16[1024,1024]{1,0:T(8,128)(2,1)S(1)} %copy-done, bf16[1024,1024]{1,0:T(8,128)(2,1)} %bitcast.302, f32[1024]{0:T(1024)S(1)} %copy-done.76), kind=kOutput, calls=%fused_computation.73 | convolution fusion | flops 4322230272 | bytes 12587008 | tf_op jit(solution)/shard_map/tf,df->td/dot_general | solution.py:355
  401.6 4.5 constant_dynamic-slice_fusion.7
  415.0 5.5 collective-permute-done.33.far
  434.1 10.8 %collective-permute-done.23 = bf16[256,1024]{0,1:T(8,128)(2,1)S(1)} collective-permute-done((bf16[256,1024]{0,1:T(8,128)(2,1)S(1)}, bf16[256,1024]{0,1:T(8,128)(2,1)S(1)}, u32[]{:S(2)}, u32[]{:S(2)}) %collective-permute-start.23) | collective-permute-done | bytes 524320 | tf_op jit(solution)/shard_map/ppermute | solution.py:162
  445.2 9.3 %collective-permute-done.21 = bf16[256,1024]{0,1:T(8,128)(2,1)S(1)} collective-permute-done((bf16[256,1024]{0,1:T(8,128)(2,1)S(1)}, bf16[256,1024]{0,1:T(8,128)(2,1)S(1)}, u32[]{:S(2)}, u32[]{:S(2)}) %collective-permute-start.21) | collective-permute-done | bytes 524320 | tf_op jit(solution)/shard_map/ppermute | solution.py:162
  479.7 4.7 collective-permute-done.35.side
  485.1 32.9 %shard_map.399 = bf16[8,128,512]{2,1,0:T(8,128)(2,1)} custom-call(bf16[128,512]{1,0:T(8,128)(2,1)} %copy-done.23, bf16[128,512]{1,0:T(8,128)(2,1)} %collective-permute-done.33.far, bf16[2,128,512]{2,1,0:T(8,128)(2,1)} %collective-permute-done.34.near, bf16[128,512]{1,0:T(8,128)(2,1)} %copy-done.62, bf16[3,128,512]{2,1,0:T(8,128)(2,1)} %collective-permute-done.36.side_rest), custom_call_target="tpu_custom_call" | custom-call | tf_op jit(solution)/shard_map/pallas_call | solution.py:189
  523.9 7.1 %multiply_reduce_fusion = (f32[4,512]{1,0:T(4,128)S(1)}, f32[4,512,1024]{2,1,0:T(8,128)}) fusion(f32[4,512,1024]{2,1,0:T(8,128)} %copy-done.1, f32[4,512]{1,0:T(4,128)S(1)} %get-tuple-element.153, bf16[512,4,64]{0,2,1:T(8,128)(2,1)S(1)} %slice.264, bf16[1024,3,4,64]{0,3,2,1:T(8,128)(2,1)} %bitcast.285), kind=kOutput, calls=%fused_computation.1 | convolution fusion | flops 274724864 | bytes 17580032 | tf_op jit(solution)/shard_map/qhe,khe->hqk/dot_general | solution.py:119
  539.2 5.8 fusion.60
  607.3 7.3 %collective-permute-done.27 = bf16[256,1024]{0,1:T(8,128)(2,1)S(1)} collective-permute-done((bf16[256,1024]{0,1:T(8,128)(2,1)S(1)}, bf16[256,1024]{0,1:T(8,128)(2,1)S(1)}, u32[]{:S(2)}, u32[]{:S(2)}) %collective-permute-start.27) | collective-permute-done | bytes 524320 | tf_op jit(solution)/shard_map/ppermute | solution.py:162
  (394 shorter events, 200.1 us)
Async XLA Ops:
  5.2 14.4 %collective-permute-start = (bf16[432,256]{1,0:T(8,128)(2,1)}, bf16[432,256]{1,0:T(8,128)(2,1)S(1)}, u32[]{:S(2)}, u32[]{:S(2)}) collective-permute-start(bf16[432,256]{1,0:T(8,128)(2,1)} %get-tuple-element.183.own), channel_id=1, source_target_pairs={{0,16},{4,20},{8,24},{12,28},{16,0},{20,4},{24,8},{28,12},{1,17},{... | collective-permute-start | bytes 663560 | tf_op jit(solution)/shard_map/ppermute | solution.py:162
  9.3 103.4 %collective-permute-start.2 = (bf16[432,256]{1,0:T(8,128)(2,1)}, bf16[432,256]{1,0:T(8,128)(2,1)}, u32[]{:S(2)}, u32[]{:S(2)}) collective-permute-start(bf16[432,256]{1,0:T(8,128)(2,1)} %get-tuple-element.183.own), channel_id=1, source_target_pairs={{0,4},{4,0},{8,12},{12,8},{16,20},{20,16},{24,28},{28,24},{1,5},{5... | collective-permute-start | bytes 663560 | tf_op jit(solution)/shard_map/ppermute | solution.py:162
  19.7 29.5 %collective-permute-start.1 = (bf16[2,432,256]{2,1,0:T(8,128)(2,1)S(1)}, bf16[2,432,256]{2,1,0:T(8,128)(2,1)S(1)}, u32[]{:S(2)}, u32[]{:S(2)}) collective-permute-start(bf16[2,432,256]{2,1,0:T(8,128)(2,1)S(1)} %pad_maximum_fusion.10), channel_id=1, source_target_pairs={{0,8},{4,12},{8,0},{12,4},{16,24},{20,28},{24,16},{28,20},{1,9},{5... | collective-permute-start | bytes 1327112 | tf_op jit(solution)/shard_map/ppermute | solution.py:162
  28.4 18.1 %collective-permute-start.5 = (bf16[2,256,256]{2,1,0:T(8,128)(2,1)S(1)}, bf16[2,256,256]{2,1,0:T(8,128)(2,1)S(1)}, u32[]{:S(2)}, u32[]{:S(2)}) collective-permute-start(bf16[2,256,256]{2,1,0:T(8,128)(2,1)S(1)} %pad_maximum_fusion.15), channel_id=1, source_target_pairs={{0,8},{4,12},{8,0},{12,4},{16,24},{20,28},{24,16},{28,20},{1,9},{5... | collective-permute-start | bytes 786440 | tf_op jit(solution)/shard_map/ppermute | solution.py:162
  29.7 18.5 %collective-permute-start.12 = (bf16[128,1024]{1,0:T(8,128)(2,1)S(1)}, bf16[128,1024]{1,0:T(8,128)(2,1)S(1)}, u32[]{:S(2)}, u32[]{:S(2)}) collective-permute-start(bf16[128,1024]{1,0:T(8,128)(2,1)S(1)} %copy-done.39), channel_id=1, source_target_pairs={{0,16},{4,20},{8,24},{12,28},{16,0},{20,4},{24,8},{28,12},{1,17},{... | collective-permute-start | bytes 786440 | tf_op jit(solution)/shard_map/ppermute | solution.py:162
  46.6 27.3 %collective-permute-start.7 = (bf16[3,256,256]{2,1,0:T(8,128)(2,1)S(1)}, bf16[3,256,256]{2,1,0:T(8,128)(2,1)}, u32[]{:S(2)}, u32[]{:S(2)}) collective-permute-start(bf16[3,256,256]{2,1,0:T(8,128)(2,1)S(1)} %pad_maximum_fusion.11), channel_id=1, source_target_pairs={{0,4},{4,0},{8,12},{12,8},{16,20},{20,16},{24,28},{28,24},{1,5},{5... | collective-permute-start | bytes 1179656 | tf_op jit(solution)/shard_map/ppermute | solution.py:162
  50.2 62.5 %collective-permute-start.3 = (bf16[3,432,256]{2,1,0:T(8,128)(2,1)}, bf16[3,432,256]{2,1,0:T(8,128)(2,1)}, u32[]{:S(2)}, u32[]{:S(2)}) collective-permute-start(bf16[3,432,256]{2,1,0:T(8,128)(2,1)} %pad_maximum_fusion.5), channel_id=1, source_target_pairs={{0,4},{4,0},{8,12},{12,8},{16,20},{20,16},{24,28},{28,24},{1,5},{5... | collective-permute-start | bytes 1990664 | tf_op jit(solution)/shard_map/ppermute | solution.py:162
  51.6 22.4 %collective-permute-start.6 = (bf16[256,256]{1,0:T(8,128)(2,1)S(1)}, bf16[256,256]{1,0:T(8,128)(2,1)S(1)}, u32[]{:S(2)}, u32[]{:S(2)}) collective-permute-start(bf16[256,256]{1,0:T(8,128)(2,1)S(1)} %pad_maximum_fusion.21.own), channel_id=1, source_target_pairs={{0,4},{4,0},{8,12},{12,8},{16,20},{20,16},{24,28},{28,24},{1,5},{5... | collective-permute-start | bytes 393224 | tf_op jit(solution)/shard_map/ppermute | solution.py:162
  62.2 136.3 %collective-permute-start.17 = (bf16[2,128,1024]{2,1,0:T(8,128)(2,1)}, bf16[2,128,1024]{2,1,0:T(8,128)(2,1)}, u32[]{:S(2)}, u32[]{:S(2)}) collective-permute-start(bf16[2,128,1024]{2,1,0:T(8,128)(2,1)} %pad_maximum_fusion.7), channel_id=1, source_target_pairs={{0,8},{4,12},{8,0},{12,4},{16,24},{20,28},{24,16},{28,20},{1,9},{5... | collective-permute-start | bytes 1572872 | tf_op jit(solution)/shard_map/ppermute | solution.py:162
  73.9 130.2 %collective-permute-start.14 = (bf16[2,128,1024]{2,1,0:T(8,128)(2,1)}, bf16[2,128,1024]{2,1,0:T(8,128)(2,1)}, u32[]{:S(2)}, u32[]{:S(2)}) collective-permute-start(bf16[2,128,1024]{2,1,0:T(8,128)(2,1)} %pad_maximum_fusion.6), channel_id=1, source_target_pairs={{0,8},{4,12},{8,0},{12,4},{16,24},{20,28},{24,16},{28,20},{1,9},{5... | collective-permute-start | bytes 1572872 | tf_op jit(solution)/shard_map/ppermute | solution.py:162
  111.1 90.9 %collective-permute-start.10 = (bf16[1024,256]{1,0:T(8,128)(2,1)}, bf16[1024,256]{1,0:T(8,128)(2,1)}, u32[]{:S(2)}, u32[]{:S(2)}) collective-permute-start(bf16[1024,256]{1,0:T(8,128)(2,1)} %bitcast.310), channel_id=1, source_target_pairs={{0,2},{1,3},{2,0},{3,1},{4,6},{5,7},{6,4},{7,5},{8,10},{9,11},{10,... | collective-permute-start | bytes 1572872 | tf_op jit(solution)/shard_map/ppermute | solution.py:162
  200.5 41.6 %collective-permute-start.19 = (bf16[3,128,1024]{2,1,0:T(8,128)(2,1)}, bf16[3,128,1024]{2,1,0:T(8,128)(2,1)}, u32[]{:S(2)}, u32[]{:S(2)}) collective-permute-start(bf16[3,128,1024]{2,1,0:T(8,128)(2,1)} %pad_maximum_fusion.4), channel_id=1, source_target_pairs={{0,4},{4,0},{8,12},{12,8},{16,20},{20,16},{24,28},{28,24},{1,5},{5... | collective-permute-start | bytes 2359304 | tf_op jit(solution)/shard_map/ppermute | solution.py:162
  204.2 167.5 %collective-permute-start.11 = (bf16[2,1024,256]{2,1,0:T(8,128)(2,1)}, bf16[2,1024,256]{2,1,0:T(8,128)(2,1)}, u32[]{:S(2)}, u32[]{:S(2)}) collective-permute-start(bf16[2,1024,256]{2,1,0:T(8,128)(2,1)} %pad_maximum_fusion.1), channel_id=1, source_target_pairs={{0,1},{1,0},{2,3},{3,2},{4,5},{5,4},{6,7},{7,6},{8,9},{9,8},{10,11... | collective-permute-start | bytes 3145736 | tf_op jit(solution)/shard_map/ppermute | solution.py:162
  206.2 100.7 %collective-permute-start.16 = (bf16[3,128,1024]{2,1,0:T(8,128)(2,1)}, bf16[3,128,1024]{2,1,0:T(8,128)(2,1)}, u32[]{:S(2)}, u32[]{:S(2)}) collective-permute-start(bf16[3,128,1024]{2,1,0:T(8,128)(2,1)} %pad_maximum_fusion.3), channel_id=1, source_target_pairs={{0,4},{4,0},{8,12},{12,8},{16,20},{20,16},{24,28},{28,24},{1,5},{5... | collective-permute-start | bytes 2359304 | tf_op jit(solution)/shard_map/ppermute | solution.py:162
  211.1 161.9 %collective-permute-start.9 = (bf16[2,1024,256]{1,2,0:T(8,128)(2,1)}, bf16[2,1024,256]{1,2,0:T(8,128)(2,1)}, u32[]{:S(2)}, u32[]{:S(2)}) collective-permute-start(bf16[2,1024,256]{1,2,0:T(8,128)(2,1)} %pad_maximum_fusion.2), channel_id=1, source_target_pairs={{0,1},{1,0},{2,3},{3,2},{4,5},{5,4},{6,7},{7,6},{8,9},{9,8},{10,11... | collective-permute-start | bytes 3145736 | tf_op jit(solution)/shard_map/ppermute | solution.py:162
  211.1 29.4 %collective-permute-start.18 = (bf16[128,1024]{1,0:T(8,128)(2,1)S(1)}, bf16[128,1024]{1,0:T(8,128)(2,1)S(1)}, u32[]{:S(2)}, u32[]{:S(2)}) collective-permute-start(bf16[128,1024]{1,0:T(8,128)(2,1)S(1)} %copy-done.40), channel_id=1, source_target_pairs={{0,4},{4,0},{8,12},{12,8},{16,20},{20,16},{24,28},{28,24},{1,5},{5... | collective-permute-start | bytes 786440 | tf_op jit(solution)/shard_map/ppermute | solution.py:162
  240.5 66.3 %collective-permute-start.15 = (bf16[128,1024]{1,0:T(8,128)(2,1)}, bf16[128,1024]{1,0:T(8,128)(2,1)}, u32[]{:S(2)}, u32[]{:S(2)}) collective-permute-start(bf16[128,1024]{1,0:T(8,128)(2,1)} %own), channel_id=1, source_target_pairs={{0,4},{4,0},{8,12},{12,8},{16,20},{20,16},{24,28},{28,24},{1,5},{5... | collective-permute-start | bytes 786440 | tf_op jit(solution)/shard_map/ppermute | solution.py:162
  408.3 19.8 %collective-permute-start.22 = (bf16[2,256,1024]{1,2,0:T(8,128)(2,1)}, bf16[2,256,1024]{1,2,0:T(8,128)(2,1)}, u32[]{:S(2)}, u32[]{:S(2)}) collective-permute-start(bf16[2,256,1024]{1,2,0:T(8,128)(2,1)} %bitcast.320), channel_id=1, source_target_pairs={{0,1},{1,0},{2,3},{3,2},{4,5},{5,4},{6,7},{7,6},{8,9},{9,8},{10,11... | collective-permute-start | bytes 3145736 | tf_op jit(solution)/shard_map/ppermute | solution.py:162
  410.6 21.0 %collective-permute-start.20 = (bf16[2,256,1024]{1,2,0:T(8,128)(2,1)}, bf16[2,256,1024]{1,2,0:T(8,128)(2,1)}, u32[]{:S(2)}, u32[]{:S(2)}) collective-permute-start(bf16[2,256,1024]{1,2,0:T(8,128)(2,1)} %bitcast.319), channel_id=1, source_target_pairs={{0,1},{1,0},{2,3},{3,2},{4,5},{5,4},{6,7},{7,6},{8,9},{9,8},{10,11... | collective-permute-start | bytes 3145736 | tf_op jit(solution)/shard_map/ppermute | solution.py:162
  422.2 37.4 %collective-permute-start.34 = (bf16[2,128,512]{2,1,0:T(8,128)(2,1)}, bf16[2,128,512]{2,1,0:T(8,128)(2,1)}, u32[]{:S(2)}, u32[]{:S(2)}) collective-permute-start(bf16[2,128,512]{2,1,0:T(8,128)(2,1)} %pad_maximum_fusion.20), channel_id=1, source_target_pairs={{0,8},{4,12},{8,0},{12,4},{16,24},{20,28},{24,16},{28,20},{1,9},{5... | collective-permute-start | bytes 786440 | tf_op jit(solution)/shard_map/ppermute | solution.py:162
  430.0 14.9 %collective-permute-start.23 = (bf16[256,1024]{0,1:T(8,128)(2,1)S(1)}, bf16[256,1024]{0,1:T(8,128)(2,1)S(1)}, u32[]{:S(2)}, u32[]{:S(2)}) collective-permute-start(bf16[256,1024]{0,1:T(8,128)(2,1)S(1)} %fusion.88), channel_id=1, source_target_pairs={{0,2},{1,3},{2,0},{3,1},{4,6},{5,7},{6,4},{7,5},{8,10},{9,11},{10,... | collective-permute-start | bytes 1572872 | tf_op jit(solution)/shard_map/ppermute | solution.py:162
  433.1 21.4 %collective-permute-start.21 = (bf16[256,1024]{0,1:T(8,128)(2,1)S(1)}, bf16[256,1024]{0,1:T(8,128)(2,1)S(1)}, u32[]{:S(2)}, u32[]{:S(2)}) collective-permute-start(bf16[256,1024]{0,1:T(8,128)(2,1)S(1)} %fusion.87), channel_id=1, source_target_pairs={{0,2},{1,3},{2,0},{3,1},{4,6},{5,7},{6,4},{7,5},{8,10},{9,11},{10,... | collective-permute-start | bytes 1572872 | tf_op jit(solution)/shard_map/ppermute | solution.py:162
  461.3 23.8 %collective-permute-start.36 = (bf16[3,128,512]{2,1,0:T(8,128)(2,1)}, bf16[3,128,512]{2,1,0:T(8,128)(2,1)}, u32[]{:S(2)}, u32[]{:S(2)}) collective-permute-start(bf16[3,128,512]{2,1,0:T(8,128)(2,1)} %pad_maximum_fusion.12), channel_id=1, source_target_pairs={{0,4},{4,0},{8,12},{12,8},{16,20},{20,16},{24,28},{28,24},{1,5},{5... | collective-permute-start | bytes 1179656 | tf_op jit(solution)/shard_map/ppermute | solution.py:162
  466.3 52.8 %collective-permute-start.25 = (bf16[2,256,256]{2,1,0:T(8,128)(2,1)}, bf16[2,256,256]{2,1,0:T(8,128)(2,1)}, u32[]{:S(2)}, u32[]{:S(2)}) collective-permute-start(bf16[2,256,256]{2,1,0:T(8,128)(2,1)} %pad_maximum_fusion.17), channel_id=1, source_target_pairs={{0,1},{1,0},{2,3},{3,2},{4,5},{5,4},{6,7},{7,6},{8,9},{9,8},{10,11... | collective-permute-start | bytes 786440 | tf_op jit(solution)/shard_map/ppermute | solution.py:162
  (95 other events, 2043.2 us)
